TPU v7x, 32 devices: a whole 2x2x4 slice. The times are simulated.
32 devices in a mesh: groups: 2 (over x), expert: 8 (over z, y), seq: 2 (over core).
Axes of the slice: x: 2, y: 2, z: 4, core: 2. Of those that a mesh axis runs over, the one named last changes fastest.
Arguments:
- query: bfloat16 [16, 128, 1024], P(('groups', 'expert')), parts along dimension 0, may hold values from -160 to 160
- key_cache: bfloat16 [16, 768, 1024], P(('groups', 'expert'), 'seq'), parts along dimension 0, may hold values from -4 to 4
- value_cache: bfloat16 [16, 768, 1024], P(('groups', 'expert'), 'seq'), parts along dimension 0, may hold values from -6 to 6
- key_new: bfloat16 [16, 128, 1024], P(('groups', 'expert')), parts along dimension 0, may hold values from -6 to 6
- value_new: bfloat16 [16, 128, 1024], P(('groups', 'expert')), parts along dimension 0, may hold values from -6 to 6
- resid: bfloat16 [16, 128, 1024], P(('groups', 'expert')), parts along dimension 0, may hold values from -6 to 6
- routing: int32 [16, 128, 1], P(('groups', 'expert')), parts along dimension 0, may hold values from 0 to 7; in each aligned block of 128 rows (0 to 127, 128 to 255, ..., all dimensions but the last counted through in order) at most 48 rows name the same one
- router_prob: float32 [16, 128], P(('groups', 'expert')), parts along dimension 0, may hold values from 0.2 to 1
- out_weight: bfloat16 [1024, 1024], replicated, may hold values from -0.1875 to 0.1875
- ffn_gain: float32 [1024], replicated, may hold values from 0.5 to 2
- w_gate: bfloat16 [8, 1024, 2560], P('expert', None, 'seq'), may hold values from -0.1875 to 0.1875
- w_up: bfloat16 [8, 1024, 2560], P('expert', None, 'seq'), may hold values from -0.1875 to 0.1875
- w_down: bfloat16 [8, 2560, 1024], P('expert', 'seq'), may hold values from -0.125 to 0.125
Outputs:
- layer_out: bfloat16 [16, 128, 1024], P(('groups', 'expert')), parts along dimension 0
There are 2 independent parts, one for each index of `groups`. A program takes and returns all parts, laid end to end along the dimension named above; an argument that names none is the same for every part. Nothing has to cross between parts.
Inputs may be any that keep to these rules, and one draw needn't show every extreme that they name: `routing`: among the 128 tokens of one sequence no expert is named more than 48 times, a bound that some block reaches.
All inputs are finite; a program needn't handle non-finite values.
Results may differ from a plain program's by a relative error of at most 0.014.
Values may be sent and summed in bfloat16 or wider, within the bound.
A program may use at most 64 MiB of HBM per device.

v0:
```python
import math

import jax
import jax.numpy as jnp
from jax import lax
from jax.sharding import PartitionSpec as P

HEADS = 16
HEAD_DIM = 64


def rescale(weighted, factor):
    token_rows = weighted.shape[0]
    shaped = weighted.reshape(token_rows, HEADS, HEAD_DIM) * jnp.transpose(factor)[:, :, None]
    return shaped.reshape(token_rows, HEADS * HEAD_DIM)


def join(first, runner_expert):
    peak = jnp.maximum(first[0], runner_expert[0])
    left = jnp.exp(first[0] - peak)
    right = jnp.exp(runner_expert[0] - peak)
    denom = first[1] * left + runner_expert[1] * right
    weighted = rescale(first[2], left) + rescale(runner_expert[2], right)
    return (peak, denom, weighted)


def partial_attend(heads_q, keys, values, allowed):
    scale = 1.0 / math.sqrt(HEAD_DIM)
    keys_h = keys.reshape(-1, HEADS, HEAD_DIM)
    values_h = values.reshape(-1, HEADS, HEAD_DIM)
    scores = jnp.einsum("qhd,khd->hqk", heads_q, keys_h, preferred_element_type=jnp.float32) * scale
    if allowed is not None:
        scores = jnp.where(allowed[None], scores, -jnp.inf)
    peak = jnp.max(scores, axis=2)
    expw = jnp.exp(scores - peak[:, :, None])
    denom = jnp.sum(expw, axis=2)
    weights = expw.astype(jnp.bfloat16)
    weighted = jnp.einsum("hqk,khd->qhd", weights, values_h, preferred_element_type=jnp.float32)
    return (peak, denom, weighted.reshape(heads_q.shape[0], HEADS * HEAD_DIM))


def on_device(
    query,
    key_cache,
    value_cache,
    key_new,
    value_new,
    resid,
    routing,
    router_prob,
    out_weight,
    ffn_gain,
    w_gate,
    w_up,
    w_down,
):
    tokens = query.shape[1]
    width = query.shape[2]
    heads_q = query[0].reshape(tokens, HEADS, HEAD_DIM)
    cached = partial_attend(heads_q, key_cache[0], value_cache[0], None)
    stacked = (
        lax.all_gather(cached[0][None], "seq", axis=0, tiled=True),
        lax.all_gather(cached[1][None], "seq", axis=0, tiled=True),
        lax.all_gather(cached[2][None], "seq", axis=0, tiled=True),
    )
    merged = (stacked[0][0], stacked[1][0], stacked[2][0])
    merged = join(merged, (stacked[0][1], stacked[1][1], stacked[2][1]))
    causal = jnp.arange(tokens)[None, :] <= jnp.arange(tokens)[:, None]
    fresh = partial_attend(heads_q, key_new[0], value_new[0], causal)
    final = join(merged, fresh)
    attn = rescale(final[2], 1.0 / final[1]).astype(jnp.bfloat16)
    projected = jnp.dot(attn, out_weight, preferred_element_type=jnp.float32)
    hidden = (resid[0].astype(jnp.float32) + projected).astype(jnp.bfloat16)
    hidden_f = hidden.astype(jnp.float32)
    meansq = jnp.mean(hidden_f * hidden_f, axis=-1, keepdims=True)
    normed = (hidden_f * lax.rsqrt(meansq + 1e-06) * ffn_gain).astype(jnp.bfloat16)
    experts = lax.axis_size("expert")
    capacity = max(2, 3 * tokens // experts)
    route = routing[0, :, 0]
    onehot = (route[:, None] == jnp.arange(experts, dtype=jnp.int32)[None, :]).astype(jnp.float32)
    lower = (jnp.arange(tokens)[None, :] <= jnp.arange(tokens)[:, None]).astype(jnp.float32)
    running = jnp.dot(lower, onehot, preferred_element_type=jnp.float32)
    rank = (jnp.sum(running * onehot, axis=1) - 1.0).astype(jnp.int32)
    target = route * capacity + rank
    placer = (jnp.arange(experts * capacity, dtype=jnp.int32)[:, None] == target[None, :]).astype(
        jnp.bfloat16
    )
    outgoing = jnp.dot(placer, normed, preferred_element_type=jnp.float32).astype(jnp.bfloat16)
    outgoing = outgoing.reshape(experts, capacity, width)
    arrived = lax.all_to_all(outgoing, "expert", split_axis=0, concat_axis=0, tiled=True)
    sources, count, features = arrived.shape
    token_rows = arrived.reshape(sources * count, features)
    gate = jnp.dot(token_rows, w_gate[0], preferred_element_type=jnp.float32)
    upper = jnp.dot(token_rows, w_up[0], preferred_element_type=jnp.float32)
    act = (jax.nn.gelu(gate, approximate=True) * upper).astype(jnp.bfloat16)
    expert_result = jnp.dot(act, w_down[0], preferred_element_type=jnp.float32).reshape(
        sources, count, features
    )
    finished = lax.psum_scatter(
        expert_result.astype(jnp.bfloat16), "seq", scatter_dimension=2, tiled=True
    )
    share = lax.all_to_all(finished, "expert", split_axis=0, concat_axis=0, tiled=True)
    returned = lax.all_gather(share, "seq", axis=2, tiled=True)
    returned = returned.reshape(experts * capacity, width)
    expert_out = jnp.einsum("sq,sd->qd", placer, returned, preferred_element_type=jnp.float32)
    result = hidden_f + router_prob[0][:, None] * expert_out
    return result.astype(jnp.bfloat16)[None]


def solution(mesh):
    in_specs = (
        P(("groups", "expert"), None, None),
        P(("groups", "expert"), "seq", None),
        P(("groups", "expert"), "seq", None),
        P(("groups", "expert"), None, None),
        P(("groups", "expert"), None, None),
        P(("groups", "expert"), None, None),
        P(("groups", "expert"), None, None),
        P(("groups", "expert"), None),
        P(),
        P(),
        P("expert", None, "seq"),
        P("expert", None, "seq"),
        P("expert", "seq", None),
    )
    out_specs = P(("groups", "expert"), None, None)
    return jax.shard_map(
        on_device, mesh=mesh, in_specs=in_specs, out_specs=out_specs, check_vma=False
    )
```

profile of v0, /device:TPU:1, one launch (start us, length us, event | category | flops | bytes accessed | tf_op | source)
XLA Modules:
  0.0 105.6 jit_solution(5618038022987506223)
XLA Ops:
  6.5 1.9 %copy.27 = bf16[1,128,1024]{1,2,0:T(8,128)(2,1)} copy(bf16[1,128,1024]{2,1,0:T(8,128)(2,1)} %param.13) | data formatting | bytes 524288 | tf_op args[0]
  8.5 1.5 %copy.28 = bf16[1,384,1024]{1,2,0:T(8,128)(2,1)S(1)} copy(bf16[1,384,1024]{2,1,0:T(8,128)(2,1)} %param.14) | data formatting | bytes 1572864 | tf_op args[1]
  10.0 2.3 %copy.29 = bf16[1,384,1024]{1,2,0:T(8,128)(2,1)} copy(bf16[1,384,1024]{2,1,0:T(8,128)(2,1)} %param.15) | data formatting | bytes 1572864 | tf_op args[2]
  12.3 1.7 %multiply_reduce_fusion = (f32[16,128]{1,0:T(8,128)S(1)}, f32[16,128,384]{2,1,0:T(8,128)S(1)}) fusion(bf16[128,16,64]{0,2,1:T(8,128)(2,1)} %bitcast.73, bf16[384,16,64]{0,2,1:T(8,128)(2,1)S(1)} %bitcast.69), kind=kOutput, calls=%fused_computation.2 | convolution fusion | flops 102234112 | bytes 4202496 | tf_op jit(solution)/shard_map/qhd,khd->hqk/dot_general | solution.py:31
  14.0 1.6 %copy-done.1 = f32[16,128,384]{2,1,0:T(8,128)} copy-done((f32[16,128,384]{2,1,0:T(8,128)}, f32[16,128,384]{2,1,0:T(8,128)S(1)}, u32[]{:S(2)}) %copy-start.1) | copy-done | bytes 3145752
  15.6 1.1 %fusion.17 = f32[16,128,64]{1,2,0:T(8,128)S(1)} fusion(bf16[384,16,64]{0,2,1:T(8,128)(2,1)S(1)} %bitcast.72, f32[16,128,384]{2,1,0:T(8,128)S(1)} %get-tuple-element.14, f32[16,128]{1,0:T(8,128)S(1)} %get-tuple-element.13), kind=kOutput, calls=%fused_computation.19 | convolution fusion | flops 103022592 | bytes 4464640 | tf_op jit(solution)/shard_map/hqk,khd->qhd/dot_general | solution.py:38
  16.8 1.0 copy.30
  17.9 2.7 %fusion.6 = f32[16,128]{1,0:T(8,128)S(1)} fusion(f32[16,128,384]{2,1,0:T(8,128)} %copy-done.1, f32[16,128]{1,0:T(8,128)S(1)} %get-tuple-element.13), kind=kLoop, calls=%fused_computation.10 | loop fusion | flops 2357248 | bytes 3162112 | tf_op jit(solution)/shard_map/reduce_sum | solution.py:36
  20.6 1.8 %all-gather = f32[32,128]{1,0:T(8,128)S(1)} all-gather(f32[16,128]{1,0:T(8,128)S(1)} %get-tuple-element.13), channel_id=2, replica_groups=mesh['groups'=2,'expert'=8,'seq'=2] {'seq'}, dimensions={0}, use_global_device_ids=true | all-gather | bytes 24576 | tf_op jit(solution)/shard_map/all_gather | solution.py:62
  22.4 1.8 %all-gather.1 = f32[32,128]{1,0:T(8,128)S(1)} all-gather(f32[16,128]{1,0:T(8,128)S(1)} %fusion.6), channel_id=3, replica_groups=mesh['groups'=2,'expert'=8,'seq'=2] {'seq'}, dimensions={0}, use_global_device_ids=true | all-gather | bytes 24576 | tf_op jit(solution)/shard_map/all_gather | solution.py:63
  24.2 0.2 copy.33
  24.4 1.1 %copy.34 = bf16[1,128,1024]{1,2,0:T(8,128)(2,1)S(1)} copy(bf16[1,128,1024]{2,1,0:T(8,128)(2,1)} %param.17) | data formatting | bytes 524288 | tf_op args[4]
  25.7 0.4 fusion.57
  26.1 1.0 copy-done.2
  27.3 2.2 %all-gather.4.cloned.1.call-done = f32[2,128,1024]{2,1,0:T(8,128)} async-done(((f32[1,128,1024]{2,1,0:T(8,128)}), f32[2,128,1024]{2,1,0:T(8,128)}) %all-gather.4.cloned.1.call-update) | async-done | bytes 1048592 | tf_op jit(solution)/shard_map/all_gather | solution.py:64
  29.4 2.3 %fusion.56 = (f32[1,128,1024]{2,1,0:T(8,128)}, f32[1,128,1024]{2,1,0:T(8,128)}) fusion(f32[2,128,1024]{2,1,0:T(8,128)} %all-gather.4.cloned.1.call-done), kind=kLoop, calls=%fused_computation.75 | loop fusion | bytes 2097152 | tf_op jit(solution)/shard_map/slice | solution.py:66
  31.8 1.2 %copy.31 = f32[1,128,1024]{1,2,0:T(8,128)S(1)} copy(f32[1,128,1024]{2,1,0:T(8,128)} %get-tuple-element.7) | data formatting | bytes 1048576 | tf_op jit(solution)/shard_map/slice | solution.py:66
  33.0 2.0 %copy.32 = f32[1,128,1024]{1,2,0:T(8,128)} copy(f32[1,128,1024]{2,1,0:T(8,128)} %get-tuple-element.8) | data formatting | bytes 1048576 | tf_op jit(solution)/shard_map/slice | solution.py:67
  35.0 1.8 %fusion.30 = bf16[128,16,64]{0,2,1:T(8,128)(2,1)S(1)} fusion(bf16[128,16,64]{0,2,1:T(8,128)(2,1)S(1)} %bitcast.79, f32[16,128,128]{1,2,0:T(8,128)} %copy-done.2, f32[16,128]{1,0:T(8,128)S(1)} %get-tuple-element.15, f32[128,16,64]{0,2,1:T(8,128)} %bitcast.77, f32[128,16,64]{0,2,1:T(8,128)S(1)} %bitcast.76, f32[128,16]{0,1:T(8,128)S(1)} %get-tuple-element.10, ...), kind=kOutput, calls=%fused_computation.34 | convolution fusion | flops 35127296 | bytes 2670592 | tf_op jit(solution)/shard_map/hqk,khd->qhd/dot_general | solution.py:38
  36.8 0.3 copy-done.5
  37.1 0.5 multiply_reduce_fusion.1
  37.7 0.4 convolution_convert_fusion
  38.1 24.8 %all_to_all.10 = bf16[8,48,1024]{2,1,0:T(8,128)(2,1)S(1)} all-to-all(bf16[8,48,1024]{2,1,0:T(8,128)(2,1)S(1)} %bitcast.70), channel_id=1, replica_groups=mesh['groups'=2,'expert'=8,'seq'=2] {'expert'}, dimensions={0} | all-to-all | bytes 1572864 | tf_op jit(solution)/shard_map/all_to_all | solution.py:90
  62.9 1.4 %fusion.14 = f32[384,1280]{1,0:T(8,128)S(1)} fusion(bf16[384,1024]{1,0:T(8,128)(2,1)S(1)} %bitcast.81, bf16[1,1024,1280]{2,1,0:T(8,128)(2,1)S(1)} %copy-done), kind=kOutput, calls=%fused_computation.18 | convolution fusion | flops 1010565120 | bytes 5373952 | tf_op jit(solution)/shard_map/dot_general | solution.py:93
  64.3 0.3 copy-done.10
  64.6 1.2 %fusion = bf16[384,1280]{1,0:T(8,128)(2,1)S(1)} fusion(f32[384,1280]{1,0:T(8,128)S(1)} %fusion.14, bf16[384,1024]{1,0:T(8,128)(2,1)S(1)} %bitcast.82, bf16[1,1024,1280]{2,1,0:T(8,128)(2,1)S(1)} %copy-done.10), kind=kOutput, calls=%fused_computation.4 | convolution fusion | flops 1007616000 | bytes 6356992 | tf_op jit(solution)/shard_map/dot_general | solution.py:94
  65.8 0.5 copy-done.11
  66.4 2.1 %fusion.21 = bf16[8,48,1024]{2,1,0:T(8,128)(2,1)} fusion(bf16[8,48,1280]{2,1,0:T(8,128)(2,1)S(1)} %bitcast.85, bf16[1,1280,1024]{2,1,0:T(8,128)(2,1)S(1)} %copy-done.11), kind=kOutput, calls=%fused_computation.22 | convolution fusion | flops 1007026176 | bytes 4390912 | tf_op jit(solution)/shard_map/dot_general | solution.py:96
  68.5 8.7 %reduce-scatter.2.cloned.1.call-done = bf16[8,48,512]{2,1,0:T(8,128)(2,1)} async-done(((bf16[8,48,1024]{2,1,0:T(8,128)(2,1)}), bf16[8,48,512]{2,1,0:T(8,128)(2,1)}) %reduce-scatter.2.cloned.1.call-update) | async-done | bytes 393232 | tf_op jit(solution)/shard_map/reduce_scatter | solution.py:99
  77.1 16.9 %all_to_all.11 = bf16[8,48,512]{2,1,0:T(8,128)(2,1)S(1)} all-to-all(bf16[8,48,512]{2,1,0:T(8,128)(2,1)} %reduce-scatter.2.cloned.1.call-done), channel_id=1, replica_groups=mesh['groups'=2,'expert'=8,'seq'=2] {'expert'}, dimensions={0} | all-to-all | bytes 786432 | tf_op jit(solution)/shard_map/all_to_all | solution.py:102
  94.1 3.7 %all_gather.15 = bf16[8,48,1024]{2,1,0:T(8,128)(2,1)S(1)} all-gather(bf16[8,48,512]{2,1,0:T(8,128)(2,1)S(1)} %all_to_all.11), channel_id=1, replica_groups=mesh['groups'=2,'expert'=8,'seq'=2] {'seq'}, dimensions={2}, use_global_device_ids=true | all-gather | bytes 1179648 | tf_op jit(solution)/shard_map/all_gather | solution.py:103
  97.7 1.1 fusion.33
  (32 shorter events, 0.5 us)
Async XLA Ops:
  6.5 56.3 %copy-start = (bf16[1,1024,1280]{2,1,0:T(8,128)(2,1)S(1)}, bf16[1,1024,1280]{2,1,0:T(8,128)(2,1)}, u32[]{:S(2)}) copy-start(bf16[1,1024,1280]{2,1,0:T(8,128)(2,1)} %param.23) | copy-start | bytes 7864324
  6.5 22.9 %all-gather.4.cloned.1.call-start = ((), (), s32[]{:S(2)}) async-start(), calls=%async_computation.3 | async-start | bytes 1572864 | tf_op jit(solution)/shard_map/all_gather | solution.py:64
  12.3 3.4 %copy-start.3 = (bf16[1,384,1024]{1,2,0:T(8,128)(2,1)S(1)}, bf16[1,384,1024]{1,2,0:T(8,128)(2,1)}, u32[]{:S(2)}) copy-start(bf16[1,384,1024]{1,2,0:T(8,128)(2,1)} %copy.29) | copy-start | bytes 2359300
  14.0 1.6 %copy-start.1 = (f32[16,128,384]{2,1,0:T(8,128)}, f32[16,128,384]{2,1,0:T(8,128)S(1)}, u32[]{:S(2)}) copy-start(f32[16,128,384]{2,1,0:T(8,128)S(1)} %get-tuple-element.14) | copy-start | bytes 9437188
  16.7 7.5 %copy-start.6 = (bf16[1,128,1024]{2,1,0:T(8,128)(2,1)S(1)}, bf16[1,128,1024]{2,1,0:T(8,128)(2,1)}, u32[]{:S(2)}) copy-start(bf16[1,128,1024]{2,1,0:T(8,128)(2,1)} %param.16) | copy-start | bytes 786436
  17.8 7.8 %copy-start.12 = (s32[1,128,1]{1,2,0:T(1,128)S(1)}, s32[1,128,1]{1,2,0:T(1,128)}, u32[]{:S(2)}) copy-start(s32[1,128,1]{1,2,0:T(1,128)} %param.19) | copy-start | bytes 1540
  17.8 7.9 %copy-start.4 = (bf16[1,128,1024]{1,2,0:T(8,128)(2,1)S(1)}, bf16[1,128,1024]{1,2,0:T(8,128)(2,1)}, u32[]{:S(2)}) copy-start(bf16[1,128,1024]{1,2,0:T(8,128)(2,1)} %copy.27) | copy-start | bytes 786436
  17.8 59.3 %reduce-scatter.2.cloned.1.call-start = ((), (), s32[]{:S(2)}) async-start(), calls=%async_computation.4 | async-start | bytes 1179648 | tf_op jit(solution)/shard_map/reduce_scatter | solution.py:99
  26.1 1.0 copy-start.2
  35.0 2.1 %copy-start.5 = (bf16[1024,1024]{1,0:T(8,128)(2,1)S(1)}, bf16[1024,1024]{1,0:T(8,128)(2,1)}, u32[]{:S(2)}) copy-start(bf16[1024,1024]{1,0:T(8,128)(2,1)} %param.21) | copy-start | bytes 6291460
  35.0 2.1 %copy-start.7 = (bf16[1,128,1024]{2,1,0:T(8,128)(2,1)S(1)}, bf16[1,128,1024]{2,1,0:T(8,128)(2,1)}, u32[]{:S(2)}) copy-start(bf16[1,128,1024]{2,1,0:T(8,128)(2,1)} %param.18) | copy-start | bytes 786436
  35.0 2.6 %copy-start.8 = (f32[1024]{0:T(1024)S(1)}, f32[1024]{0:T(1024)}, u32[]{:S(2)}) copy-start(f32[1024]{0:T(1024)} %param.22) | copy-start | bytes 12292
  62.9 1.7 %copy-start.10 = (bf16[1,1024,1280]{2,1,0:T(8,128)(2,1)S(1)}, bf16[1,1024,1280]{2,1,0:T(8,128)(2,1)}, u32[]{:S(2)}) copy-start(bf16[1,1024,1280]{2,1,0:T(8,128)(2,1)} %param.24) | copy-start | bytes 7864324
  64.6 1.7 %copy-start.11 = (bf16[1,1280,1024]{2,1,0:T(8,128)(2,1)S(1)}, bf16[1,1280,1024]{2,1,0:T(8,128)(2,1)}, u32[]{:S(2)}) copy-start(bf16[1,1280,1024]{2,1,0:T(8,128)(2,1)} %param.25) | copy-start | bytes 7864324
  68.4 29.3 %copy-start.9 = (f32[1,128]{1,0:T(1,128)S(1)}, f32[1,128]{1,0:T(1,128)}, u32[]{:S(2)}) copy-start(f32[1,128]{1,0:T(1,128)} %param.20) | copy-start | bytes 1540
Sparse Core Ops, SparseCore 0:
  17.9 11.4 all-gather.3
  68.6 8.5 reduce-scatter.1
where the time goes:
time: 107 us; the launch traced here: 106 us
  blocking collectives  49 us (46%)
  local copies, waits for them, and re-layouts  17.4 us (16%)
  between operations  13.6 us (13%)
  matrix products  11.8 us (11%)
  waiting for transfers between devices  10.9 us (10%)
  other arithmetic  2.96 us (3%)
    all_to_all x1, blocking collectives, on_device(): lax.all_to_all(outgoing, 'expert', split_axis=0, concat_axis=0, tiled=True)  24.8 us
    all_to_all x1, blocking collectives, on_device(): lax.all_to_all(finished, 'expert', split_axis=0, concat_axis=0, tiled=True)  16.9 us
    unnamed x31, local copies, waits for them, and re-layouts  10.8 us
    reduce_scatter x1, waiting for transfers between devices, on_device(): lax.psum_scatter(expert_result.astype(jnp.bfloat16), 'seq', scatter_dimen...  8.68 us
    all_gather x1, blocking collectives, on_device(): returned = lax.all_gather(share, 'seq', axis=2, tiled=True)  3.65 us
    slice x2, local copies, waits for them, and re-layouts, on_device(): merged = (stacked[0][0], stacked[1][0], stacked[2][0])  3.55 us
    dot_general x2, matrix products, partial_attend(): jnp.einsum('hqk,khd->qhd', weights, values_h, preferred_element_type=jnp....  2.9 us
    reduce_sum x2, other arithmetic, partial_attend(): denom = jnp.sum(expw, axis=2)  2.9 us
  transfers between devices with their start and end apart: 2, of which 2 were waited for; matrix products, arithmetic and copies ran while one was open for 5% of the time, Pallas kernels for 0%

commit v1 on v0

v1 whole, which is shorter than its diff:
```python
import functools
import math

import jax
import jax.numpy as jnp
from jax import lax
from jax.experimental import pallas as pl
from jax.experimental.pallas import tpu as pltpu
from jax.sharding import PartitionSpec as P

HEAD_DIM = 64
LANES = 128
MESH = pl.DeviceIdType.MESH
F32 = jnp.float32
BF16 = jnp.bfloat16


def flip(me, k):
    other, bit = me, 1
    while bit <= k:
        if k & bit:
            other = other + bit - 2 * bit * ((me // bit) % 2)
        bit *= 2
    return other


def kernel(
    cfg,
    q_hbm,
    kc_hbm,
    vc_hbm,
    kn_hbm,
    vn_hbm,
    res_hbm,
    route_ref,
    prob_ref,
    wo_hbm,
    gain_ref,
    wg_hbm,
    wu_hbm,
    wd_hbm,
    out_ref,
    q,
    kc,
    vc,
    kn,
    vn,
    res,
    wo,
    wg,
    wu,
    wd,
    o_loc,
    o_send,
    o_recv,
    o_fresh,
    st_send,
    st_recv,
    attn,
    sendb,
    xb,
    act,
    rs_send,
    rs_recv,
    ret,
    yb,
    in_sem,
    chunk_sem,
    o_sem,
    st_sem,
    disp_sem,
    fwd_sem,
    rs_sem,
    ret_sem,
    yfwd_sem,
):
    experts, capp, groups, chunks, tile = cfg
    tokens, width = q.shape
    half = width // 2
    slots = experts * capp
    hidden_units = wg.shape[1]
    heads = width // HEAD_DIM
    span = width // chunks
    me = lax.axis_index("expert")
    core = lax.axis_index("seq")
    partner = 1 - core

    def load(src, dst, sem):
        copy = pltpu.make_async_copy(src, dst, sem)
        copy.start()
        return copy

    in_chunks = []
    for j in range(chunks):
        cols = pl.ds(j * span, span)
        in_chunks.append(
            [
                load(q_hbm.at[0, :, cols], q.at[:, cols], chunk_sem.at[0, j]),
                load(kc_hbm.at[0, :, cols], kc.at[:, cols], chunk_sem.at[1, j]),
                load(vc_hbm.at[0, :, cols], vc.at[:, cols], chunk_sem.at[2, j]),
            ]
        )

    barrier = pltpu.get_barrier_semaphore()
    pl.semaphore_signal(barrier, inc=1, device_id={"seq": partner}, device_id_type=MESH)
    for k in range(1, experts):
        pl.semaphore_signal(
            barrier, inc=1, device_id={"expert": flip(me, k)}, device_id_type=MESH
        )

    loads = {}
    for i, (name, src, dst) in enumerate(
        (
            ("kn", kn_hbm.at[0], kn),
            ("vn", vn_hbm.at[0], vn),
            ("res", res_hbm.at[0], res),
            ("wo", wo_hbm, wo),
            ("wg", wg_hbm.at[0], wg),
            ("wu", wu_hbm.at[0], wu),
            ("wd", wd_hbm.at[0], wd),
        )
    ):
        loads[name] = load(src, dst, in_sem.at[i])

    route = route_ref[...]
    row_i = lax.broadcasted_iota(jnp.int32, (tokens, tokens), 0)
    col_i = lax.broadcasted_iota(jnp.int32, (tokens, tokens), 1)
    upto = (row_i <= col_i).astype(F32).astype(BF16)
    named = lax.broadcasted_iota(jnp.int32, (experts, tokens), 0) == route
    onehot = named.astype(F32)
    running = jnp.dot(onehot.astype(BF16), upto, preferred_element_type=F32)
    target = jnp.sum(running * onehot, axis=0, keepdims=True) - 1.0
    for k in range(1, experts):
        target = target + jnp.where(route == flip(me, k), float(k * capp), 0.0)
    eye = row_i == col_i
    target_col = jnp.sum(jnp.where(eye, target, 0.0), axis=1, keepdims=True)
    prob_col = jnp.sum(jnp.where(eye, prob_ref[...], 0.0), axis=1, keepdims=True)
    placer = (
        (lax.broadcasted_iota(jnp.int32, (slots, tokens), 0).astype(F32) == target)
        .astype(F32)
        .astype(BF16)
    )
    placer_t = (
        (lax.broadcasted_iota(jnp.int32, (tokens, slots), 1).astype(F32) == target_col)
        .astype(F32)
        .astype(BF16)
    )

    scale = 1.0 / math.sqrt(HEAD_DIM)
    lane = lax.broadcasted_iota(jnp.int32, (tokens, LANES), 1)
    low = lane < HEAD_DIM
    mask_a = jnp.where(low, scale, 0.0).astype(BF16)
    mask_b = jnp.where(low, 0.0, scale).astype(BF16)
    causal = col_i <= row_i
    causal = jnp.concatenate([causal.astype(F32)] * 2, axis=0) > 0.5

    def attend(p, keys, values, masked, peaks, sums):
        cols = slice(p * LANES, (p + 1) * LANES)
        both = q[:, cols]
        both = jnp.concatenate([both * mask_a, both * mask_b], axis=0)
        scores = lax.dot_general(
            both, keys[:, cols], (((1,), (1,)), ((), ())), preferred_element_type=F32
        )
        if masked:
            scores = jnp.where(causal, scores, -jnp.inf)
        peak = jnp.max(scores, axis=1, keepdims=True)
        expw = jnp.exp(scores - peak)
        total = jnp.sum(expw, axis=1, keepdims=True)
        weighted = jnp.dot(expw.astype(BF16), values[:, cols], preferred_element_type=F32)
        weighted = jnp.where(low, weighted[:tokens], weighted[tokens:])
        for i in range(2):
            rows = slice(i * tokens, (i + 1) * tokens)
            peaks = jnp.where(lane == 2 * p + i, peak[rows], peaks)
            sums = jnp.where(lane == 2 * p + i, total[rows], sums)
        return weighted, peaks, sums

    pairs = heads // 2
    per_chunk = pairs // chunks
    peak_loc = jnp.zeros((tokens, LANES), F32)
    sum_loc = jnp.ones((tokens, LANES), F32)
    o_copies = []
    for j in range(chunks):
        for copy in in_chunks[j]:
            copy.wait()
        for i in range(per_chunk):
            p = j * per_chunk + i
            weighted, peak_loc, sum_loc = attend(p, kc, vc, False, peak_loc, sum_loc)
            o_loc[:, p * LANES : (p + 1) * LANES] = weighted
            o_send[j, :, i * LANES : (i + 1) * LANES] = weighted.astype(BF16)
        if j == 0:
            pl.semaphore_wait(barrier, experts)
        copy = pltpu.make_async_remote_copy(
            src_ref=o_send.at[j],
            dst_ref=o_recv.at[j],
            send_sem=o_sem.at[0, j],
            recv_sem=o_sem.at[1, j],
            device_id={"seq": partner},
            device_id_type=MESH,
        )
        copy.start()
        o_copies.append(copy)
    st_send[...] = jnp.where(lane < HEAD_DIM, peak_loc, pltpu.roll(sum_loc, HEAD_DIM, 1))
    st_copy = pltpu.make_async_remote_copy(
        src_ref=st_send,
        dst_ref=st_recv,
        send_sem=st_sem.at[0],
        recv_sem=st_sem.at[1],
        device_id={"seq": partner},
        device_id_type=MESH,
    )
    st_copy.start()

    loads["kn"].wait()
    loads["vn"].wait()
    peak_new = jnp.zeros((tokens, LANES), F32)
    sum_new = jnp.ones((tokens, LANES), F32)
    for p in range(pairs):
        weighted, peak_new, sum_new = attend(p, kn, vn, True, peak_new, sum_new)
        o_fresh[:, p * LANES : (p + 1) * LANES] = weighted

    st_copy.wait()
    other = st_recv[...]
    peak_rem = other
    sum_rem = pltpu.roll(other, HEAD_DIM, 1)
    peak = jnp.maximum(jnp.maximum(peak_loc, peak_rem), peak_new)
    f_loc = jnp.exp(peak_loc - peak)
    f_rem = jnp.exp(peak_rem - peak)
    f_new = jnp.exp(peak_new - peak)
    inv = 1.0 / (f_loc * sum_loc + f_rem * sum_rem + f_new * sum_new)
    f_loc, f_rem, f_new = f_loc * inv, f_rem * inv, f_new * inv
    for j in range(chunks):
        o_copies[j].wait()
        for i in range(per_chunk):
            p = j * per_chunk + i
            cols = slice(p * LANES, (p + 1) * LANES)

            def spread(f):
                return jnp.where(low, f[:, 2 * p : 2 * p + 1], f[:, 2 * p + 1 : 2 * p + 2])

            value = (
                spread(f_loc) * o_loc[:, cols]
                + spread(f_rem) * o_recv[j, :, i * LANES : (i + 1) * LANES].astype(F32)
                + spread(f_new) * o_fresh[:, cols]
            )
            attn[:, cols] = value.astype(BF16)

    loads["wo"].wait()
    loads["res"].wait()
    projected = jnp.dot(attn[...], wo[...], preferred_element_type=F32)
    hidden = (res[...].astype(F32) + projected).astype(BF16)
    res[...] = hidden
    hidden_f = hidden.astype(F32)
    meansq = jnp.mean(hidden_f * hidden_f, axis=-1, keepdims=True)
    normed = (hidden_f * lax.rsqrt(meansq + 1e-06) * gain_ref[...]).astype(BF16)

    outgoing = jnp.dot(placer, normed, preferred_element_type=F32).astype(BF16)
    for h in range(2):
        block = outgoing[:, h * half : (h + 1) * half].reshape(experts, capp, half)
        sendb[h] = block
        xb[h, 0] = block[0]

    def remote(src, dst, sems, k, device):
        copy = pltpu.make_async_remote_copy(
            src_ref=src,
            dst_ref=dst,
            send_sem=sems.at[0, k],
            recv_sem=sems.at[1, k],
            device_id=device,
            device_id_type=MESH,
        )
        copy.start()
        return copy

    sent = {}
    for k in range(1, experts):
        sent[k] = remote(
            sendb.at[core, k], xb.at[core, k], disp_sem, k, {"expert": flip(me, k)}
        )
    loads["wg"].wait()
    loads["wu"].wait()
    loads["wd"].wait()

    returned = {}
    pending = []
    for g, (k0, k1) in enumerate(groups):
        rows = (k1 - k0) * capp
        forwarded = []
        for k in range(max(k0, 1), k1):
            sent[k].wait_recv()
            forwarded.append(
                remote(xb.at[core, k], xb.at[core, k], fwd_sem, k, {"seq": partner})
            )
        for copy in forwarded:
            copy.wait_recv()
        pending += forwarded

        def hidden_tile(t, carry):
            cols = pl.ds(pl.multiple_of(t * tile, tile), tile)
            left = xb[0, k0:k1].reshape(rows, half)
            right = xb[1, k0:k1].reshape(rows, half)
            x = jnp.concatenate([left, right], axis=1)
            gate = jnp.dot(x, wg[:, cols], preferred_element_type=F32)
            upper = jnp.dot(x, wu[:, cols], preferred_element_type=F32)
            act[:rows, cols] = (jax.nn.gelu(gate, approximate=True) * upper).astype(BF16)
            return carry

        lax.fori_loop(0, hidden_units // tile, hidden_tile, 0)
        theirs = pl.ds(pl.multiple_of(partner * half, half), half)
        mine = pl.ds(pl.multiple_of(core * half, half), half)
        here = pl.ds(k0 * capp, rows)
        rs_send[here, :] = jnp.dot(
            act[:rows], wd[:, theirs], preferred_element_type=F32
        ).astype(BF16)
        swap = remote(rs_send.at[here], rs_recv.at[here], rs_sem, g, {"seq": partner})
        own = jnp.dot(act[:rows], wd[:, mine], preferred_element_type=F32)
        swap.wait_recv()
        pending.append(swap)
        own = (own + rs_recv[here, :].astype(F32)).astype(BF16)
        ret[k0:k1] = own.reshape(k1 - k0, capp, half)
        for k in range(max(k0, 1), k1):
            returned[k] = remote(
                ret.at[k], yb.at[core, k], ret_sem, k, {"expert": flip(me, k)}
            )
        if k0 == 0:
            yb[core, 0] = ret[0]
            last = [remote(ret.at[0], yb.at[core, 0], yfwd_sem, 0, {"seq": partner})]

    for k in range(1, experts):
        returned[k].wait_recv()
        last.append(remote(yb.at[core, k], yb.at[core, k], yfwd_sem, k, {"seq": partner}))
    for copy in last:
        copy.wait_recv()
    y = jnp.concatenate([yb[0].reshape(slots, half), yb[1].reshape(slots, half)], axis=1)
    expert_out = jnp.dot(placer_t, y, preferred_element_type=F32)
    out_ref[...] = (res[...].astype(F32) + prob_col * expert_out).astype(BF16)
    for k in range(1, experts):
        sent[k].wait_send()
        returned[k].wait_send()
    for copy in pending + last:
        copy.wait_send()


def on_device(*args):
    (query, key_cache, value_cache, key_new, value_new, resid, routing, router_prob) = args[:8]
    (out_weight, ffn_gain, w_gate, w_up, w_down) = args[8:]
    tokens, width = query.shape[1:]
    context = key_cache.shape[1]
    hidden_units = w_gate.shape[2]
    experts = lax.axis_size("expert")
    capacity = max(2, 3 * tokens // experts)
    capp = -(-capacity // 16) * 16
    half = width // 2
    slots = experts * capp
    chunks = 4
    tile = 256 if hidden_units % 256 == 0 else 128
    groups = ((0, experts // 2), (experts // 2, experts))
    most = max(b - a for a, b in groups) * capp
    vmem = pl.BlockSpec(memory_space=pltpu.VMEM)
    hbm = pl.BlockSpec(memory_space=pl.ANY)
    dma = pltpu.SemaphoreType.DMA
    out = pl.pallas_call(
        functools.partial(kernel, (experts, capp, groups, chunks, tile)),
        out_shape=jax.ShapeDtypeStruct((tokens, width), BF16),
        in_specs=[hbm] * 6 + [vmem] * 2 + [hbm, vmem] + [hbm] * 3,
        out_specs=vmem,
        scratch_shapes=[
            pltpu.VMEM((tokens, width), BF16),
            pltpu.VMEM((context, width), BF16),
            pltpu.VMEM((context, width), BF16),
            pltpu.VMEM((tokens, width), BF16),
            pltpu.VMEM((tokens, width), BF16),
            pltpu.VMEM((tokens, width), BF16),
            pltpu.VMEM((width, width), BF16),
            pltpu.VMEM((width, hidden_units), BF16),
            pltpu.VMEM((width, hidden_units), BF16),
            pltpu.VMEM((hidden_units, width), BF16),
            pltpu.VMEM((tokens, width), F32),
            pltpu.VMEM((chunks, tokens, width // chunks), BF16),
            pltpu.VMEM((chunks, tokens, width // chunks), BF16),
            pltpu.VMEM((tokens, width), F32),
            pltpu.VMEM((tokens, LANES), F32),
            pltpu.VMEM((tokens, LANES), F32),
            pltpu.VMEM((tokens, width), BF16),
            pltpu.VMEM((2, experts, capp, half), BF16),
            pltpu.VMEM((2, experts, capp, half), BF16),
            pltpu.VMEM((most, hidden_units), BF16),
            pltpu.VMEM((slots, half), BF16),
            pltpu.VMEM((slots, half), BF16),
            pltpu.VMEM((experts, capp, half), BF16),
            pltpu.VMEM((2, experts, capp, half), BF16),
            dma((7,)),
            dma((3, chunks)),
            dma((2, chunks)),
            dma((2,)),
            dma((2, experts)),
            dma((2, experts)),
            dma((2, len(groups))),
            dma((2, experts)),
            dma((2, experts)),
        ],
        compiler_params=pltpu.CompilerParams(
            collective_id=0, has_side_effects=True, vmem_limit_bytes=60 * 1024 * 1024
        ),
    )(
        query,
        key_cache,
        value_cache,
        key_new,
        value_new,
        resid,
        routing.reshape(1, tokens),
        router_prob,
        out_weight,
        ffn_gain.reshape(1, width),
        w_gate,
        w_up,
        w_down,
    )
    return out[None]


def solution(mesh):
    in_specs = (
        P(("groups", "expert"), None, None),
        P(("groups", "expert"), "seq", None),
        P(("groups", "expert"), "seq", None),
        P(("groups", "expert"), None, None),
        P(("groups", "expert"), None, None),
        P(("groups", "expert"), None, None),
        P(("groups", "expert"), None, None),
        P(("groups", "expert"), None),
        P(),
        P(),
        P("expert", None, "seq"),
        P("expert", None, "seq"),
        P("expert", "seq", None),
    )
    out_specs = P(("groups", "expert"), None, None)
    return jax.shard_map(
        on_device, mesh=mesh, in_specs=in_specs, out_specs=out_specs, check_vma=False
    )
```

time: 107 us -> 42.4 us (0.40); the launches traced: 106 us -> 42.2 us
  blocking collectives: 49 us -> 0 us
  Pallas kernels: 0 us -> 40.5 us
  local copies, waits for them, and re-layouts: 17.4 us -> 1.67 us
  between operations: 13.6 us -> 0.01 us
  matrix products: 11.8 us -> 0 us
  waiting for transfers between devices: 10.9 us -> 0 us
  other arithmetic: 2.96 us -> 0 us
    all_to_all x2 -> x0, blocking collectives: 41.7 us -> none  [the longest x1 24.8 us: on_device(): lax.all_to_all(outgoing, 'expert', split_axis=0, concat_axis=0, tiled=True)]
    pallas_call x0 -> x1, Pallas kernels: none -> 40.5 us  [on_device(): pl.pallas_call(functools.partial(kernel, (experts, capp, groups, chunks,...]
    dot_general x11 -> x0, matrix products: 11.8 us -> none  [the longest x2 2.9 us: partial_attend(): jnp.einsum('hqk,khd->qhd', weights, values_h, preferred_element_type=jnp....]
    unnamed x31 -> x1, local copies, waits for them, and re-layouts: 10.8 us -> 1.67 us
    reduce_scatter x1 -> x0, waiting for transfers between devices: 8.68 us -> none  [on_device(): lax.psum_scatter(expert_result.astype(jnp.bfloat16), 'seq', scatter_dimen...]
    all_gather x3 -> x0, blocking collectives: 7.28 us -> none  [the longest x1 3.65 us: on_device(): returned = lax.all_gather(share, 'seq', axis=2, tiled=True)]
    slice x3 -> x0, local copies, waits for them, and re-layouts: 5.58 us -> none  [the longest x2 3.55 us: on_device(): merged = (stacked[0][0], stacked[1][0], stacked[2][0])]
    reduce_sum x2 -> x0, other arithmetic: 2.9 us -> none  [partial_attend(): denom = jnp.sum(expw, axis=2)]
  transfers between devices with their start and end apart: 2 -> 0, of which waited for: 2 -> 0; matrix products, arithmetic and copies ran while one was open for 5% -> 0% of each run, Pallas kernels for 0% -> 0%
where the time goes in v1:
time: 42.4 us; the launch traced here: 42.2 us
  Pallas kernels  40.5 us (96%)
  local copies, waits for them, and re-layouts  1.67 us (4%)
    pallas_call x1, Pallas kernels, on_device(): pl.pallas_call(functools.partial(kernel, (experts, capp, groups, chunks,...  40.5 us
    unnamed x1, local copies, waits for them, and re-layouts  1.67 us

profile of v1, /device:TPU:1, one launch (start us, length us, event | category | flops | bytes accessed | tf_op | source)
XLA Modules:
  0.0 42.2 jit_solution(9477598382332917651)
XLA Ops:
  0.0 40.5 %shard_map.127 = bf16[128,1024]{1,0:T(8,128)(2,1)} custom-call(bf16[1,128,1024]{2,1,0:T(8,128)(2,1)} %q_hbm.1, bf16[1,384,1024]{2,1,0:T(8,128)(2,1)} %kc_hbm.1, bf16[1,384,1024]{2,1,0:T(8,128)(2,1)} %vc_hbm.1, bf16[1,128,1024]{2,1,0:T(8,128)(2,1)} %kn_hbm.1, bf16[1,128,1024]{2,1,0:T(8,128)(2,1)} %vn_hbm.1, bf16[1,128,1024]{2,1,0:T(8,128)(2,1)} %res_hbm.1, ...), custom_call_target="tpu_custom_call" | custom-call | tf_op jit(solution)/shard_map/pallas_call | solution.py:361
  40.5 1.7 %copy.15 = bf16[1,128,1024]{2,1,0:T(8,128)(2,1)} copy(bf16[1,128,1024]{2,1,0:T(8,128)(2,1)} %bitcast.3) | data formatting | bytes 524288

commit v2 on v1

--- a/solution.py
+++ b/solution.py
@@ -65,7 +65,7 @@
     ret,
     yb,
     in_sem,
-    chunk_sem,
+    first_sem,
     o_sem,
     st_sem,
     disp_sem,
@@ -80,7 +80,6 @@
     slots = experts * capp
     hidden_units = wg.shape[1]
     heads = width // HEAD_DIM
-    span = width // chunks
     me = lax.axis_index("expert")
     core = lax.axis_index("seq")
     partner = 1 - core
@@ -90,16 +89,11 @@
         copy.start()
         return copy
 
-    in_chunks = []
-    for j in range(chunks):
-        cols = pl.ds(j * span, span)
-        in_chunks.append(
-            [
-                load(q_hbm.at[0, :, cols], q.at[:, cols], chunk_sem.at[0, j]),
-                load(kc_hbm.at[0, :, cols], kc.at[:, cols], chunk_sem.at[1, j]),
-                load(vc_hbm.at[0, :, cols], vc.at[:, cols], chunk_sem.at[2, j]),
-            ]
-        )
+    first = [
+        load(q_hbm.at[0], q, first_sem.at[0]),
+        load(kc_hbm.at[0], kc, first_sem.at[1]),
+        load(vc_hbm.at[0], vc, first_sem.at[2]),
+    ]
 
     barrier = pltpu.get_barrier_semaphore()
     pl.semaphore_signal(barrier, inc=1, device_id={"seq": partner}, device_id_type=MESH)
@@ -179,9 +173,9 @@
     peak_loc = jnp.zeros((tokens, LANES), F32)
     sum_loc = jnp.ones((tokens, LANES), F32)
     o_copies = []
+    for copy in first:
+        copy.wait()
     for j in range(chunks):
-        for copy in in_chunks[j]:
-            copy.wait()
         for i in range(per_chunk):
             p = j * per_chunk + i
             weighted, peak_loc, sum_loc = attend(p, kc, vc, False, peak_loc, sum_loc)
@@ -294,17 +288,17 @@
             copy.wait_recv()
         pending += forwarded
 
-        def hidden_tile(t, carry):
-            cols = pl.ds(pl.multiple_of(t * tile, tile), tile)
+        def hidden_tile(t):
+            cols = pl.ds(t * tile, tile)
             left = xb[0, k0:k1].reshape(rows, half)
             right = xb[1, k0:k1].reshape(rows, half)
             x = jnp.concatenate([left, right], axis=1)
             gate = jnp.dot(x, wg[:, cols], preferred_element_type=F32)
             upper = jnp.dot(x, wu[:, cols], preferred_element_type=F32)
             act[:rows, cols] = (jax.nn.gelu(gate, approximate=True) * upper).astype(BF16)
-            return carry
-
-        lax.fori_loop(0, hidden_units // tile, hidden_tile, 0)
+
+        for t in range(hidden_units // tile):
+            hidden_tile(t)
         theirs = pl.ds(pl.multiple_of(partner * half, half), half)
         mine = pl.ds(pl.multiple_of(core * half, half), half)
         here = pl.ds(k0 * capp, rows)
@@ -351,9 +345,9 @@
     capp = -(-capacity // 16) * 16
     half = width // 2
     slots = experts * capp
-    chunks = 4
+    chunks = 2
     tile = 256 if hidden_units % 256 == 0 else 128
-    groups = ((0, experts // 2), (experts // 2, experts))
+    groups = ((0, experts // 2), (experts // 2, 3 * experts // 4), (3 * experts // 4, experts))
     most = max(b - a for a, b in groups) * capp
     vmem = pl.BlockSpec(memory_space=pltpu.VMEM)
     hbm = pl.BlockSpec(memory_space=pl.ANY)
@@ -389,7 +383,7 @@
             pltpu.VMEM((experts, capp, half), BF16),
             pltpu.VMEM((2, experts, capp, half), BF16),
             dma((7,)),
-            dma((3, chunks)),
+            dma((3,)),
             dma((2, chunks)),
             dma((2,)),
             dma((2, experts)),

time: 42.4 us -> 38.5 us (0.908)
  Pallas kernels: 40.5 us -> 36.6 us
    pallas_call x1, Pallas kernels: 40.5 us -> 36.6 us  [on_device(): pl.pallas_call(functools.partial(kernel, (experts, capp, groups, chunks,...]
where the time goes in v2:
time: 38.5 us; the launch traced here: 38.3 us
  Pallas kernels  36.6 us (95%)
  local copies, waits for them, and re-layouts  1.67 us (4%)
    pallas_call x1, Pallas kernels, on_device(): pl.pallas_call(functools.partial(kernel, (experts, capp, groups, chunks,...  36.6 us
    unnamed x1, local copies, waits for them, and re-layouts  1.67 us

profile of v2, /device:TPU:1, one launch (start us, length us, event | category | flops | bytes accessed | tf_op | source)
XLA Modules:
  0.0 38.3 jit_solution(1236394459198485803)
XLA Ops:
  0.0 36.6 %shard_map.127 = bf16[128,1024]{1,0:T(8,128)(2,1)} custom-call(bf16[1,128,1024]{2,1,0:T(8,128)(2,1)} %q_hbm.1, bf16[1,384,1024]{2,1,0:T(8,128)(2,1)} %kc_hbm.1, bf16[1,384,1024]{2,1,0:T(8,128)(2,1)} %vc_hbm.1, bf16[1,128,1024]{2,1,0:T(8,128)(2,1)} %kn_hbm.1, bf16[1,128,1024]{2,1,0:T(8,128)(2,1)} %vn_hbm.1, bf16[1,128,1024]{2,1,0:T(8,128)(2,1)} %res_hbm.1, ...), custom_call_target="tpu_custom_call" | custom-call | tf_op jit(solution)/shard_map/pallas_call | solution.py:355
  36.6 1.7 %copy.15 = bf16[1,128,1024]{2,1,0:T(8,128)(2,1)} copy(bf16[1,128,1024]{2,1,0:T(8,128)(2,1)} %bitcast.3) | data formatting | bytes 524288
